TPU v7x, 32 devices: a whole 2x2x4 slice. The times are simulated.
32 devices in a mesh: leaf: 8 (over y, x, core), rows: 4 (over z).
Axes of the slice: x: 2, y: 2, z: 4, core: 2. Of those that a mesh axis runs over, the one named last changes fastest.
Arguments:
- right_side: float32 [8, 2, 64, 512], P('leaf', None, None, 'rows'), as said below
- diag_inverse: float32 [8, 2, 512, 128], P('leaf', None, 'rows'), as said below
- sep_lower: float32 [8, 2, 512, 512], P('leaf', None, 'rows'), as said below
- front_lower: float32 [8, 2, 1024, 512], P('leaf', None, None, 'rows'), as said below
- front_index: int32 [8, 2, 1024], P('leaf'), may hold values from 0 to 1535, as said below
Outputs:
- solution: float32 [8, 2, 64, 512], P('leaf', None, None, 'rows')
- top_update: float32 [8, 2, 64, 512], P('leaf', None, None, 'rows')
Inputs may be any that keep to these rules, and one draw needn't show every extreme that they name: `front_index`: for each leaf index and slot s the 1024 entries are distinct, lie below (3 - s) * 512, and are the same on all 2**s leaf indices of the slot's subtree. `right_side`: entries of slot s are the same on all 2**s leaf indices of the slot's subtree. `diag_inverse`: entries of slot s are the same on all 2**s leaf indices of the slot's subtree. `sep_lower`: entries of slot s are the same on all 2**s leaf indices of the slot's subtree. `front_lower`: entries of slot s are the same on all 2**s leaf indices of the slot's subtree.
All inputs are finite; a program needn't handle non-finite values.
Results may differ from a plain program's by a relative error of at most 0.00011.
Values sent between devices are 32-bit elements; how exact they have to be, the bound alone decides.
A program may use at most 128 MiB of HBM per device.

v0:
```python
import jax
import jax.numpy as jnp
from jax import lax
from jax.sharding import PartitionSpec as P

exact_precision = lax.Precision.HIGHEST


def partner(value, axis, apart):
    mask = 2**apart
    pairs = [(source, source ^ mask) for source in range(lax.axis_size(axis))]
    return lax.ppermute(value, axis, pairs)


def product(left, right):
    return lax.dot_general(
        left,
        right,
        (((left.ndim - 1,), (right.ndim - 1,)), ((), ())),
        precision=exact_precision,
        preferred_element_type=jnp.float32,
    )


def solve_rows(target, inverse, prefixes, width):
    solved = []
    for block, prefix in enumerate(prefixes):
        first = block * width
        total = target[:, first : first + width]
        if block > 0:
            total = total - product(jnp.concatenate(solved, axis=1), prefix)
        solved.append(product(total, inverse[first : first + width]))
    return jnp.concatenate(solved, axis=1)


def on_device(right_side, diag_inverse, sep_lower, front_lower, front_index):
    levels = right_side.shape[1]
    vectors = right_side.shape[2]
    width = right_side.shape[3]
    blocks = lax.axis_size("rows")
    here = lax.axis_index("rows")
    depth = levels + 1
    targets = right_side[0]
    inverses = diag_inverse[0]
    lowers = sep_lower[0]
    fronts = front_lower[0]
    indices = front_index[0]
    lower_all, inverse_all = (
        lax.all_gather(lowers, "rows", axis=1, tiled=True),
        lax.all_gather(inverses, "rows", axis=1, tiled=True),
    )
    prefix_rows = [
        lower_all[:, block * width : (block + 1) * width, : block * width]
        for block in range(blocks)
    ]
    pending = None
    solutions = []
    for level in range(levels):
        height = depth - level
        if level == 0:
            target = targets[0]
        else:
            pending = pending + partner(pending, "leaf", level - 1)
            target = targets[level] - pending[:, height * width :]
            pending = pending[:, : height * width]
        gathered = lax.all_gather(target, "rows", axis=1, tiled=True)
        joined = solve_rows(
            gathered, inverse_all[level], [rows[level] for rows in prefix_rows], width
        )
        own_block = lax.dynamic_slice_in_dim(joined, here * width, width, 1)
        solutions.append(own_block)
        partial_front = product(own_block, fronts[level])
        summed = lax.psum(partial_front, "rows")
        positions = jnp.arange(height * width, dtype=jnp.int32)
        wanted = positions // width * (blocks * width) + here * width + positions % width
        hits = (wanted[:, None] == indices[level][None, :]).astype(jnp.float32)
        update = product(summed, hits)
        pending = update if level == 0 else pending + update
    top = pending.reshape(vectors, 2, width).transpose(1, 0, 2)
    return (jnp.stack(solutions, axis=0)[None], top[None])


def solution(mesh):
    in_specs = (
        P("leaf", None, None, "rows"),
        P("leaf", None, "rows", None),
        P("leaf", None, "rows", None),
        P("leaf", None, None, "rows"),
        P("leaf", None, None),
    )
    out_specs = (P("leaf", None, None, "rows"), P("leaf", None, None, "rows"))
    return jax.shard_map(
        on_device, mesh=mesh, in_specs=in_specs, out_specs=out_specs, check_vma=False
    )
```

profile of v0, /device:TPU:0, one launch (start us, length us, event | category | flops | bytes accessed | tf_op | source)
XLA Modules:
  0.0 174.2 jit_solution(17245503545314237015)
XLA Ops:
  7.2 0.7 all-gather.5.cloned.1.call-update
  7.9 0.0 all-reduce.3.cloned.1.call-start
  8.0 0.8 slice.139
  8.7 15.2 %all-gather = f32[1,1,64,512]{3,2,1,0:T(8,128)S(1)} all-gather(f32[1,1,64,128]{3,2,1,0:T(8,128)S(1)} %slice.139), channel_id=2, replica_groups=mesh['leaf'=8,'rows'=4] {'rows'}, dimensions={3}, use_global_device_ids=true | all-gather | bytes 163840 | tf_op jit(solution)/shard_map/all_gather | solution.py:66
  24.0 23.7 %all-gather.1 = f32[1,2,512,128]{3,2,1,0:T(8,128)S(1)} all-gather(f32[1,2,128,128]{3,2,1,0:T(8,128)} %param.6), channel_id=3, replica_groups=mesh['leaf'=8,'rows'=4] {'rows'}, dimensions={2}, use_global_device_ids=true | all-gather | bytes 655360 | tf_op jit(solution)/shard_map/all_gather | solution.py:50
  47.7 0.2 fusion.35
  47.9 18.6 %all-gather.5.cloned.1.call-done = f32[1,2,512,512]{3,2,1,0:T(8,128)} async-done(((f32[1,2,128,512]{3,2,1,0:T(8,128)}), f32[1,2,512,512]{3,2,1,0:T(8,128)}) %all-gather.5.cloned.1.call-update) | async-done | bytes 2097168 | tf_op jit(solution)/shard_map/all_gather | solution.py:49
  66.5 1.1 convolution_subtract_fusion.2
  67.6 0.2 fusion.34
  67.9 1.2 convolution_subtract_fusion.1
  69.0 0.2 fusion.33
  69.3 1.3 convolution_subtract_fusion
  70.6 0.2 fusion.32
  70.9 1.4 fusion.8
  72.3 0.0 all-reduce.5.cloned.1.call-start
  72.4 34.6 %all-reduce.3.cloned.1.call-done = f32[64,1024]{1,0:T(8,128)} async-done(((f32[64,1024]{1,0:T(8,128)}), f32[64,1024]{1,0:T(8,128)}) %all-reduce.3.cloned.1.call-update) | async-done | bytes 262160 | tf_op jit(solution)/shard_map/psum | solution.py:73
  107.0 1.9 %fusion = f32[64,384]{1,0:T(8,128)S(1)} fusion(f32[64,1024]{1,0:T(8,128)} %all-reduce.3.cloned.1.call-done, s32[1024]{0:T(1024)S(1)} %bitcast.100, s32[384]{0:T(512)S(1)} %fusion.56), kind=kOutput, calls=%fused_computation | convolution fusion | flops 302383104 | bytes 366080 | tf_op jit(solution)/shard_map/dot_general | solution.py:16
  108.9 0.1 collective-permute-start
  109.0 1.3 collective-permute-done
  110.3 13.3 %all_gather.15 = f32[64,512]{1,0:T(8,128)S(1)} all-gather(f32[64,128]{1,0:T(8,128)S(1)} %slice_subtract_fusion.6), channel_id=1, replica_groups=mesh['leaf'=8,'rows'=4] {'rows'}, dimensions={1}, use_global_device_ids=true | all-gather | bytes 163840 | tf_op jit(solution)/shard_map/all_gather | solution.py:66
  123.7 0.2 fusion.31
  123.9 1.1 fusion.30
  125.0 0.2 fusion.29
  125.3 1.2 fusion.15
  126.4 0.2 fusion.28
  126.7 1.3 fusion.14
  128.0 0.2 fusion.27
  128.3 1.4 fusion.6
  129.7 0.6 maximum_bitcast_fusion
  130.3 35.0 %all-reduce.5.cloned.1.call-done = f32[64,1024]{1,0:T(8,128)} async-done(((f32[64,1024]{1,0:T(8,128)}), f32[64,1024]{1,0:T(8,128)}) %all-reduce.5.cloned.1.call-update) | async-done | bytes 262160 | tf_op jit(solution)/shard_map/psum | solution.py:73
  165.3 1.6 fusion.26
  167.0 0.6 copy.10
  (16 shorter events, 0.2 us)
Async XLA Ops:
  7.2 63.7 %copy-start = (f32[1,2,1024,128]{3,2,1,0:T(8,128)S(1)}, f32[1,2,1024,128]{3,2,1,0:T(8,128)}, u32[]{:S(2)}) copy-start(f32[1,2,1024,128]{3,2,1,0:T(8,128)} %param.8) | copy-start | bytes 3145732
  7.2 65.2 %copy-start.2 = (s32[1,2,1024]{2,1,0:T(2,128)S(1)}, s32[1,2,1024]{2,1,0:T(2,128)}, u32[]{:S(2)}) copy-start(s32[1,2,1024]{2,1,0:T(2,128)} %param.9) | copy-start | bytes 24580
  7.2 59.4 %all-gather.5.cloned.1.call-start = ((), (), s32[]{:S(2)}) async-start(), calls=%async_computation.2 | async-start | bytes 2621440 | tf_op jit(solution)/shard_map/all_gather | solution.py:49
  7.9 99.1 %all-reduce.3.cloned.1.call-start = ((), (), s32[]{:S(2)}) async-start(), calls=%async_computation | async-start | bytes 524288 | tf_op jit(solution)/shard_map/psum | solution.py:73
  8.7 101.6 %copy-start.1 = (f32[1,2,64,128]{3,2,1,0:T(8,128)S(1)}, f32[1,2,64,128]{3,2,1,0:T(8,128)}, u32[]{:S(2)}) copy-start(f32[1,2,64,128]{3,2,1,0:T(8,128)} %param.5) | copy-start | bytes 196612
  72.3 93.0 %all-reduce.5.cloned.1.call-start = ((), (), s32[]{:S(2)}) async-start(), calls=%async_computation.1 | async-start | bytes 524288 | tf_op jit(solution)/shard_map/psum | solution.py:73
  108.9 1.4 collective-permute-start
Sparse Core Ops, SparseCore 0:
  9.6 56.9 all-gather.4
  72.4 34.5 all-reduce.2
  129.8 35.4 all-reduce.4
where the time goes:
time: 175 us; the launch traced here: 174 us
  waiting for transfers between devices  90.3 us (52%)
  blocking collectives  52.3 us (30%)
  matrix products  15.3 us (9%)
  between operations  13.9 us (8%)
    psum x2, waiting for transfers between devices, on_device(): summed = lax.psum(partial_front, 'rows')  69.7 us
    all_gather x2, blocking collectives, on_device(): gathered = lax.all_gather(target, 'rows', axis=1, tiled=True)  28.6 us
    all_gather x1, blocking collectives, on_device(): lax.all_gather(inverses, 'rows', axis=1, tiled=True)  23.7 us
    all_gather x1, waiting for transfers between devices, on_device(): lax.all_gather(lowers, 'rows', axis=1, tiled=True)  18.6 us
    dot_general x18, matrix products, product(): lax.dot_general(left, right, (((left.ndim - 1,), (right.ndim - 1,)), ((),...  15.3 us
  transfers between devices with their start and end apart: 4, of which 4 were waited for; matrix products, arithmetic and copies ran while one was open for 1% of the time, Pallas kernels for 0%

commit v1 on v0

--- a/solution.py
+++ b/solution.py
@@ -63,7 +63,14 @@
             pending = pending + partner(pending, "leaf", level - 1)
             target = targets[level] - pending[:, height * width :]
             pending = pending[:, : height * width]
-        gathered = lax.all_gather(target, "rows", axis=1, tiled=True)
+        peers = lax.axis_size("rows")
+        route = [(i, (i + 1) % peers) for i in range(peers)]
+        shards = [target]
+        for far in range(1, peers):
+            shards = [lax.ppermute(shards[0], "rows", route), *shards]
+        out = jnp.concatenate(shards, axis=1)
+        places = (lax.axis_index("rows") + 1) * shards[-1].shape[1]
+        gathered = jnp.roll(out, places, axis=1)
         joined = solve_rows(
             gathered, inverse_all[level], [rows[level] for rows in prefix_rows], width
         )

time: 175 us -> 177 us (1.011)
  blocking collectives: 52.3 us -> 23.5 us
  waiting for transfers between devices: 90.3 us -> 117 us
  starting transfers between devices: 0.19 us -> 4.74 us
    all_gather x2 -> x0, blocking collectives: 28.6 us -> none  [on_device(): gathered = lax.all_gather(target, 'rows', axis=1, tiled=True)]
    ppermute x0 -> x6, waiting for transfers between devices: none -> 25.3 us  [on_device(): shards = [lax.ppermute(shards[0], 'rows', route), *shards]]
    ppermute x0 -> x6, starting transfers between devices: none -> 4.55 us  [on_device(): shards = [lax.ppermute(shards[0], 'rows', route), *shards]]
    all_gather x1, waiting for transfers between devices: 18.6 us -> 21.9 us  [on_device(): lax.all_gather(lowers, 'rows', axis=1, tiled=True)]
    psum x2, waiting for transfers between devices: 69.7 us -> 67.6 us  [on_device(): summed = lax.psum(partial_front, 'rows')]
  transfers between devices with their start and end apart: 4 -> 10, of which waited for: 4 -> 9; matrix products, arithmetic and copies ran while one was open for 1% -> 1% of each run, Pallas kernels for 0% -> 0%
where the time goes in v1:
time: 177 us
  waiting for transfers between devices  117 us (66%)
  blocking collectives  23.5 us (13%)
  matrix products  15.3 us (9%)
  between operations  13.9 us (8%)
  starting transfers between devices  4.74 us (3%)
    psum x2, waiting for transfers between devices, on_device(): summed = lax.psum(partial_front, 'rows')  67.6 us
    ppermute x6, waiting for transfers between devices, on_device(): shards = [lax.ppermute(shards[0], 'rows', route), *shards]  25.3 us
    all_gather x1, blocking collectives, on_device(): lax.all_gather(inverses, 'rows', axis=1, tiled=True)  23.5 us
    all_gather x1, waiting for transfers between devices, on_device(): lax.all_gather(lowers, 'rows', axis=1, tiled=True)  21.9 us
    dot_general x18, matrix products, product(): lax.dot_general(left, right, (((left.ndim - 1,), (right.ndim - 1,)), ((),...  15.3 us
    ppermute x6, starting transfers between devices, on_device(): shards = [lax.ppermute(shards[0], 'rows', route), *shards]  4.55 us
  transfers between devices with their start and end apart: 10, of which 9 were waited for; matrix products, arithmetic and copies ran while one was open for 1% of the time, Pallas kernels for 0%

profile of v1, /device:TPU:0, one launch (start us, length us, event | category | flops | bytes accessed | tf_op | source)
XLA Modules:
  0.0 176.6 jit_solution(13958070467230166612)
XLA Ops:
  7.2 0.7 all-gather.4.cloned.1.call-update
  8.0 0.8 slice_bitcast_fusion.28
  8.7 3.1 %collective-permute-start = (f32[64,128]{1,0:T(8,128)S(1)}, f32[64,128]{1,0:T(8,128)S(1)}, u32[]{:S(2)}, u32[]{:S(2)}) collective-permute-start(f32[64,128]{1,0:T(8,128)S(1)} %slice_bitcast_fusion.28), channel_id=1, source_target_pairs={{0,1},{1,2},{2,3},{3,0},{4,5},{5,6},{6,7},{7,4},{8,9},{9,10},{10,1... | collective-permute-start | bytes 98312 | tf_op jit(solution)/shard_map/ppermute | solution.py:70
  11.8 3.9 %collective-permute-done = f32[64,128]{1,0:T(8,128)S(1)} collective-permute-done((f32[64,128]{1,0:T(8,128)S(1)}, f32[64,128]{1,0:T(8,128)S(1)}, u32[]{:S(2)}, u32[]{:S(2)}) %collective-permute-start) | collective-permute-done | bytes 32800 | tf_op jit(solution)/shard_map/ppermute | solution.py:70
  15.7 5.7 %collective-permute-done.1 = f32[64,128]{1,0:T(8,128)S(1)} collective-permute-done((f32[64,128]{1,0:T(8,128)S(1)}, f32[64,128]{1,0:T(8,128)S(1)}, u32[]{:S(2)}, u32[]{:S(2)}) %collective-permute-start.1) | collective-permute-done | bytes 32800 | tf_op jit(solution)/shard_map/ppermute | solution.py:70
  21.4 23.5 %all-gather = f32[1,2,512,128]{3,2,1,0:T(8,128)S(1)} all-gather(f32[1,2,128,128]{3,2,1,0:T(8,128)} %param.8), channel_id=2, replica_groups=mesh['leaf'=8,'rows'=4] {'rows'}, dimensions={2}, use_global_device_ids=true | all-gather | bytes 655360 | tf_op jit(solution)/shard_map/all_gather | solution.py:50
  45.0 0.2 fusion.46
  45.3 21.9 %all-gather.4.cloned.1.call-done = f32[1,2,512,512]{3,2,1,0:T(8,128)} async-done(((f32[1,2,128,512]{3,2,1,0:T(8,128)}), f32[1,2,512,512]{3,2,1,0:T(8,128)}) %all-gather.4.cloned.1.call-update) | async-done | bytes 2097168 | tf_op jit(solution)/shard_map/all_gather | solution.py:49
  67.1 1.1 convolution_subtract_fusion.5
  68.2 0.2 fusion.45
  68.5 1.2 convolution_subtract_fusion.4
  69.6 0.2 fusion.44
  69.9 1.3 convolution_subtract_fusion.3
  71.2 0.2 fusion.43
  71.5 1.4 fusion.8
  73.0 34.3 %all-reduce.3.cloned.1.call-done = f32[64,1024]{1,0:T(8,128)} async-done(((f32[64,1024]{1,0:T(8,128)}), f32[64,1024]{1,0:T(8,128)}) %all-reduce.3.cloned.1.call-update) | async-done | bytes 262160 | tf_op jit(solution)/shard_map/psum | solution.py:80
  107.3 1.9 %fusion = f32[64,384]{1,0:T(8,128)S(1)} fusion(f32[64,1024]{1,0:T(8,128)} %all-reduce.3.cloned.1.call-done, s32[1024]{0:T(1024)S(1)} %bitcast.100, s32[384]{0:T(512)S(1)} %fusion.67), kind=kOutput, calls=%fused_computation | convolution fusion | flops 302383104 | bytes 366080 | tf_op jit(solution)/shard_map/dot_general | solution.py:16
  109.3 1.3 collective-permute-done.3
  110.6 1.5 collective-permute-start.4
  112.1 4.3 %collective-permute-done.4 = f32[64,128]{1,0:T(8,128)S(1)} collective-permute-done((f32[64,128]{1,0:T(8,128)S(1)}, f32[64,128]{1,0:T(8,128)S(1)}, u32[]{:S(2)}, u32[]{:S(2)}) %collective-permute-start.4) | collective-permute-done | bytes 32800 | tf_op jit(solution)/shard_map/ppermute | solution.py:70
  116.4 5.7 %collective-permute-done.5 = f32[64,128]{1,0:T(8,128)S(1)} collective-permute-done((f32[64,128]{1,0:T(8,128)S(1)}, f32[64,128]{1,0:T(8,128)S(1)}, u32[]{:S(2)}, u32[]{:S(2)}) %collective-permute-start.5) | collective-permute-done | bytes 32800 | tf_op jit(solution)/shard_map/ppermute | solution.py:70
  122.1 5.7 %collective-permute-done.6 = f32[64,128]{1,0:T(8,128)S(1)} collective-permute-done((f32[64,128]{1,0:T(8,128)S(1)}, f32[64,128]{1,0:T(8,128)S(1)}, u32[]{:S(2)}, u32[]{:S(2)}) %collective-permute-start.6) | collective-permute-done | bytes 32800 | tf_op jit(solution)/shard_map/ppermute | solution.py:70
  128.1 1.1 convolution_subtract_fusion.2
  129.5 1.2 convolution_subtract_fusion.1
  130.6 0.2 fusion.40
  130.9 1.3 convolution_subtract_fusion
  132.2 0.2 fusion.39
  132.5 1.4 fusion.6
  133.9 0.6 maximum_bitcast_fusion
  134.5 33.3 %all-reduce.5.cloned.1.call-done = f32[64,1024]{1,0:T(8,128)} async-done(((f32[64,1024]{1,0:T(8,128)}), f32[64,1024]{1,0:T(8,128)}) %all-reduce.5.cloned.1.call-update) | async-done | bytes 262160 | tf_op jit(solution)/shard_map/psum | solution.py:80
  167.8 1.6 fusion.38
  169.4 0.6 copy.10
  (28 shorter events, 1.0 us)
Async XLA Ops:
  7.2 64.3 %copy-start = (f32[1,2,1024,128]{3,2,1,0:T(8,128)S(1)}, f32[1,2,1024,128]{3,2,1,0:T(8,128)}, u32[]{:S(2)}) copy-start(f32[1,2,1024,128]{3,2,1,0:T(8,128)} %param.10) | copy-start | bytes 3145732
  7.2 65.8 %copy-start.2 = (s32[1,2,1024]{2,1,0:T(2,128)S(1)}, s32[1,2,1024]{2,1,0:T(2,128)}, u32[]{:S(2)}) copy-start(s32[1,2,1024]{2,1,0:T(2,128)} %param.11) | copy-start | bytes 24580
  7.2 60.0 %all-gather.4.cloned.1.call-start = ((), (), s32[]{:S(2)}) async-start(), calls=%async_computation.2 | async-start | bytes 2621440 | tf_op jit(solution)/shard_map/all_gather | solution.py:49
  7.9 99.4 %all-reduce.3.cloned.1.call-start = ((), (), s32[]{:S(2)}) async-start(), calls=%async_computation | async-start | bytes 524288 | tf_op jit(solution)/shard_map/psum | solution.py:80
  8.7 101.9 %copy-start.1 = (f32[1,2,64,128]{3,2,1,0:T(8,128)S(1)}, f32[1,2,64,128]{3,2,1,0:T(8,128)}, u32[]{:S(2)}) copy-start(f32[1,2,64,128]{3,2,1,0:T(8,128)} %param.7) | copy-start | bytes 196612
  8.7 7.0 %collective-permute-start = (f32[64,128]{1,0:T(8,128)S(1)}, f32[64,128]{1,0:T(8,128)S(1)}, u32[]{:S(2)}, u32[]{:S(2)}) collective-permute-start(f32[64,128]{1,0:T(8,128)S(1)} %slice_bitcast_fusion.28), channel_id=1, source_target_pairs={{0,1},{1,2},{2,3},{3,0},{4,5},{5,6},{6,7},{7,4},{8,9},{9,10},{10,1... | collective-permute-start | bytes 98312 | tf_op jit(solution)/shard_map/ppermute | solution.py:70
  15.7 5.7 %collective-permute-start.1 = (f32[64,128]{1,0:T(8,128)S(1)}, f32[64,128]{1,0:T(8,128)S(1)}, u32[]{:S(2)}, u32[]{:S(2)}) collective-permute-start(f32[64,128]{1,0:T(8,128)S(1)} %collective-permute-done), channel_id=1, source_target_pairs={{0,1},{1,2},{2,3},{3,0},{4,5},{5,6},{6,7},{7,4},{8,9},{9,10},{10,1... | collective-permute-start | bytes 98312 | tf_op jit(solution)/shard_map/ppermute | solution.py:70
  21.4 23.5 %collective-permute-start.2 = (f32[64,128]{1,0:T(8,128)S(1)}, f32[64,128]{1,0:T(8,128)S(1)}, u32[]{:S(2)}, u32[]{:S(2)}) collective-permute-start(f32[64,128]{1,0:T(8,128)S(1)} %collective-permute-done.1), channel_id=1, source_target_pairs={{0,1},{1,2},{2,3},{3,0},{4,5},{5,6},{6,7},{7,4},{8,9},{9,10},{10,1... | collective-permute-start | bytes 98312 | tf_op jit(solution)/shard_map/ppermute | solution.py:70
  72.9 94.9 %all-reduce.5.cloned.1.call-start = ((), (), s32[]{:S(2)}) async-start(), calls=%async_computation.1 | async-start | bytes 524288 | tf_op jit(solution)/shard_map/psum | solution.py:80
  109.2 1.4 collective-permute-start.3
  110.6 5.8 %collective-permute-start.4 = (f32[64,128]{1,0:T(8,128)S(1)}, f32[64,128]{1,0:T(8,128)S(1)}, u32[]{:S(2)}, u32[]{:S(2)}) collective-permute-start(f32[64,128]{1,0:T(8,128)S(1)} %slice_subtract_fusion), channel_id=1, source_target_pairs={{0,1},{1,2},{2,3},{3,0},{4,5},{5,6},{6,7},{7,4},{8,9},{9,10},{10,1... | collective-permute-start | bytes 98312 | tf_op jit(solution)/shard_map/ppermute | solution.py:70
  116.4 5.7 %collective-permute-start.5 = (f32[64,128]{1,0:T(8,128)S(1)}, f32[64,128]{1,0:T(8,128)S(1)}, u32[]{:S(2)}, u32[]{:S(2)}) collective-permute-start(f32[64,128]{1,0:T(8,128)S(1)} %collective-permute-done.4), channel_id=1, source_target_pairs={{0,1},{1,2},{2,3},{3,0},{4,5},{5,6},{6,7},{7,4},{8,9},{9,10},{10,1... | collective-permute-start | bytes 98312 | tf_op jit(solution)/shard_map/ppermute | solution.py:70
  122.1 5.7 %collective-permute-start.6 = (f32[64,128]{1,0:T(8,128)S(1)}, f32[64,128]{1,0:T(8,128)S(1)}, u32[]{:S(2)}, u32[]{:S(2)}) collective-permute-start(f32[64,128]{1,0:T(8,128)S(1)} %collective-permute-done.5), channel_id=1, source_target_pairs={{0,1},{1,2},{2,3},{3,0},{4,5},{5,6},{6,7},{7,4},{8,9},{9,10},{10,1... | collective-permute-start | bytes 98312 | tf_op jit(solution)/shard_map/ppermute | solution.py:70
Sparse Core Ops, SparseCore 0:
  9.6 57.5 all-gather.3
  73.0 34.2 all-reduce.2
  134.0 33.7 all-reduce.4
